TPU v7x, 32 devices: a whole 2x2x4 slice. The times are simulated.
32 devices in a mesh: dp: 8 (over z, x), mp: 4 (over y, core).
Axes of the slice: x: 2, y: 2, z: 4, core: 2. Of those that a mesh axis runs over, the one named last changes fastest.
Arguments:
- grads: bfloat16 [8, 4, 4096, 256], P('dp', 'mp'), may hold values from -6 to 6
- master: float32 [4, 4096, 256], P('mp', 'dp'), may hold values from -6 to 6
- m_codes: bfloat16 [4, 4096, 256], P('mp', 'dp'), may hold values from -1 to 1
- m_scale: float32 [4, 4096], P('mp', 'dp'), may hold values from 0.005 to 0.05
- v_codes: bfloat16 [4, 4096, 256], P('mp', 'dp'), may hold values from 0.049804688 to 1
- v_scale: float32 [4, 4096], P('mp', 'dp'), may hold values from 0.001 to 0.01
Outputs:
- master_out: float32 [4, 4096, 256], P('mp', 'dp')
- m_codes_out: bfloat16 [4, 4096, 256], P('mp', 'dp')
- m_scale_out: float32 [4, 4096], P('mp', 'dp')
- v_codes_out: bfloat16 [4, 4096, 256], P('mp', 'dp')
- v_scale_out: float32 [4, 4096], P('mp', 'dp')
- weights: bfloat16 [4, 4096, 256], P('mp')
All inputs are finite; a program needn't handle non-finite values. Where the computation divides by a largest or mean magnitude, that divisor is 1e-20 or more.
Results may differ from a plain program's by a relative error of at most 0.024.
Values may be sent and summed in bfloat16 or wider, within the bound.
A program may use at most 128 MiB of HBM per device.

v0:
```python
import jax
import jax.numpy as jnp
from jax import lax
from jax.sharding import PartitionSpec as P

STEP = 8


def partner(shard, axis, apart):
    return lax.ppermute(shard, axis, [(i, i ^ 1 << apart) for i in range(lax.axis_size(axis))])


def block_code(values):
    scale = (jnp.max(jnp.abs(values), axis=-1) + 1e-06).astype(jnp.bfloat16)
    levels = (values / scale.astype(jnp.float32)[..., None]).astype(jnp.bfloat16)
    return (levels, scale)


def expand(levels, scale):
    return levels.astype(jnp.float32) * scale.astype(jnp.float32)[..., None]


def state_code(values):
    scale = jnp.max(jnp.abs(values), axis=-1) + 1e-06
    return ((values / scale[..., None]).astype(jnp.bfloat16), scale)


def per_device(grads, master, m_codes, m_scale, v_codes, v_scale):
    replicas = lax.axis_size("dp")
    owned = master.shape[1]
    width = master.shape[2]
    levels, scale = block_code(grads[0, 0].astype(jnp.float32))
    codes = levels.reshape(replicas, owned, width)
    scales = scale.reshape(replicas, owned)
    position = lax.axis_index("dp")
    digits = replicas.bit_length() - 1
    total = None
    for level in range(digits):
        own_bit = position // 2**level % 2
        other_bit = 1 - own_bit
        halves = codes.reshape(codes.shape[0] // 2, 2, owned, width)
        half_scales = scales.reshape(scales.shape[0] // 2, 2, owned)
        keep_codes = lax.dynamic_index_in_dim(halves, own_bit, 1, keepdims=False)
        keep_scales = lax.dynamic_index_in_dim(half_scales, own_bit, 1, keepdims=False)
        send_codes = lax.dynamic_index_in_dim(halves, other_bit, 1, keepdims=False)
        send_scales = lax.dynamic_index_in_dim(half_scales, other_bit, 1, keepdims=False)
        got_codes, got_scales = partner((send_codes, send_scales), "dp", level)
        summed = expand(keep_codes, keep_scales) + expand(got_codes, got_scales)
        if level + 1 < digits:
            codes, scales = block_code(summed)
        else:
            total = summed[0]
    grad_mean = total / replicas
    moment_one = 0.9 * m_codes[0].astype(jnp.float32) * m_scale[0][..., None] + 0.1 * grad_mean
    moment_two = (
        0.95 * v_codes[0].astype(jnp.float32) * v_scale[0][..., None] + 0.05 * grad_mean * grad_mean
    )
    first_fix = 1.0 - 0.9**STEP
    second_fix = 1.0 - 0.95**STEP
    master_new = master[0] - 0.1 * (moment_one / first_fix) / (
        jnp.sqrt(moment_two / second_fix) + 1e-08
    )
    one_code, one_scale = state_code(moment_one)
    two_code, two_scale = state_code(moment_two)
    gathered = lax.all_gather(master_new.astype(jnp.bfloat16), "dp", axis=0, tiled=True)
    return (
        master_new[None],
        one_code[None],
        one_scale[None],
        two_code[None],
        two_scale[None],
        gathered[None],
    )


def solution(mesh):
    return jax.shard_map(
        per_device,
        mesh=mesh,
        in_specs=(
            P("dp", "mp", None, None),
            P("mp", "dp", None),
            P("mp", "dp", None),
            P("mp", "dp"),
            P("mp", "dp", None),
            P("mp", "dp"),
        ),
        out_specs=(
            P("mp", "dp", None),
            P("mp", "dp", None),
            P("mp", "dp"),
            P("mp", "dp", None),
            P("mp", "dp"),
            P("mp", None, None),
        ),
        check_vma=False,
    )
```

profile of v0, /device:TPU:0, one launch (start us, length us, event | category | flops | bytes accessed | tf_op | source)
XLA Modules:
  0.0 131.1 jit_solution(8007333866999745570)
XLA Ops:
  7.2 0.0 all-gather.2.cloned.1.call-start
  7.2 2.2 %abs_reduce_fusion = f32[4096]{0:T(1024)S(1)} fusion(bf16[1,1,4096,256]{3,2,1,0:T(8,128)(2,1)} %param.6), kind=kLoop, calls=%fused_computation.1 | loop fusion | flops 3141632 | bytes 2113536 | tf_op jit(solution)/shard_map/reduce_max | solution.py:14
  9.5 1.9 %divide_convert_fusion = bf16[4,2,512,256]{3,2,1,0:T(8,128)(2,1)S(1)} fusion(f32[4,2,512]{2,1,0:T(2,128)S(1)} %convert_element_type.167, bf16[4,2,512,256]{3,2,1,0:T(8,128)(2,1)} %bitcast.70), kind=kLoop, calls=%fused_computation | loop fusion | flops 3145728 | bytes 4210688 | tf_op jit(solution)/shard_map/convert_element_type | solution.py:15
  11.5 1.0 dynamic-slice_bitcast_fusion
  12.5 3.0 %collective-permute-start = (bf16[4,512,256]{2,1,0:T(8,128)(2,1)}, bf16[4,512,256]{2,1,0:T(8,128)(2,1)S(1)}, u32[]{:S(2)}, u32[]{:S(2)}) collective-permute-start(bf16[4,512,256]{2,1,0:T(8,128)(2,1)} %dynamic-slice_bitcast_fusion), channel_id=1, source_target_pairs={{0,4},{4,0},{8,12},{12,8},{16,20},{20,16},{24,28},{28,24},{1,5},{5... | collective-permute-start | bytes 3145736 | tf_op jit(solution)/shard_map/ppermute | solution.py:10
  15.5 0.1 collective-permute-start.1
  15.6 23.3 %collective-permute-done.1 = bf16[4,512]{1,0:T(4,128)(2,1)S(1)} collective-permute-done((bf16[4,512]{1,0:T(4,128)(2,1)S(1)}, bf16[4,512]{1,0:T(4,128)(2,1)S(1)}, u32[]{:S(2)}, u32[]{:S(2)}) %collective-permute-start.1) | collective-permute-done | bytes 4128 | tf_op jit(solution)/shard_map/ppermute | solution.py:10
  38.9 0.0 collective-permute-done
  38.9 0.0 copy-start
  38.9 1.0 abs_reduce_fusion.1
  40.0 0.0 copy-done
  40.0 0.0 copy-start.6
  40.0 2.0 %divide_convert_fusion.1 = bf16[4,512,256]{2,1,0:T(8,128)(2,1)S(1)} fusion(bf16[4,512,256]{2,1,0:T(8,128)(2,1)} %copy-done, f32[4,512]{1,0:T(4,128)S(1)} %get-tuple-element.10, f32[4,512]{1,0:T(4,128)S(1)} %convert_element_type.174, f32[4,512]{1,0:T(4,128)S(1)} %bitcast.76, bf16[4,2,512,256]{3,2,1,0:T(8,128)(2,1)S(1)} %divide_convert_fusion, s32[]{:T(128)S(6)} %select_n.54), kind=kLoop, calls=%fused_computation.4 | loop fusion | flops 3670016 | bytes 3170308 | tf_op jit(solution)/shard_map/convert_element_type | solution.py:15
  42.1 0.0 copy-start.7
  42.1 0.0 copy-start.1
  42.1 0.0 copy-start.2
  42.1 0.0 copy-start.3
  42.2 1.9 %collective-permute-start.2 = (bf16[2,512,256]{2,1,0:T(8,128)(2,1)S(1)}, bf16[2,512,256]{2,1,0:T(8,128)(2,1)S(1)}, u32[]{:S(2)}, u32[]{:S(2)}) collective-permute-start(bf16[2,512,256]{2,1,0:T(8,128)(2,1)S(1)} %dynamic-slice_bitcast_fusion.1), channel_id=1, source_target_pairs={{0,8},{4,12},{8,0},{12,4},{16,24},{20,28},{24,16},{28,20},{1,9},{5... | collective-permute-start | bytes 1572872 | tf_op jit(solution)/shard_map/ppermute | solution.py:10
  44.1 0.3 collective-permute-start.3
  44.4 0.0 copy-done.6
  44.4 11.0 %collective-permute-done.3 = bf16[2,512]{1,0:T(2,128)(2,1)S(1)} collective-permute-done((bf16[2,512]{1,0:T(2,128)(2,1)S(1)}, bf16[2,512]{1,0:T(2,128)(2,1)S(1)}, u32[]{:S(2)}, u32[]{:S(2)}) %collective-permute-start.3) | collective-permute-done | bytes 2080 | tf_op jit(solution)/shard_map/ppermute | solution.py:10
  55.4 0.0 collective-permute-done.2
  55.4 0.5 abs_reduce_fusion.2
  55.9 0.5 divide_convert_fusion.2
  56.4 2.6 %collective-permute-start.4 = (bf16[1,512,256]{2,1,0:T(8,128)(2,1)S(1)}, bf16[1,512,256]{2,1,0:T(8,128)(2,1)S(1)}, u32[]{:S(2)}, u32[]{:S(2)}) collective-permute-start(bf16[1,512,256]{2,1,0:T(8,128)(2,1)S(1)} %constant_dynamic-slice_fusion.1), channel_id=1, source_target_pairs={{0,16},{4,20},{8,24},{12,28},{16,0},{20,4},{24,8},{28,12},{1,17},{... | collective-permute-start | bytes 786440 | tf_op jit(solution)/shard_map/ppermute | solution.py:10
  59.1 0.4 collective-permute-start.5
  59.5 0.0 copy-done.7
  59.5 10.2 %collective-permute-done.5 = bf16[1,512]{1,0:T(2,128)(2,1)S(1)} collective-permute-done((bf16[1,512]{1,0:T(2,128)(2,1)S(1)}, bf16[1,512]{1,0:T(2,128)(2,1)S(1)}, u32[]{:S(2)}, u32[]{:S(2)}) %collective-permute-start.5) | collective-permute-done | bytes 1056 | tf_op jit(solution)/shard_map/ppermute | solution.py:10
  69.7 0.0 collective-permute-done.4
  69.7 0.0 copy-done.1
  69.7 0.0 copy-done.2
  69.7 0.0 copy-done.3
  69.7 1.4 %abs_reduce_fusion.3 = (f32[512]{0:T(512)S(1)}, f32[512]{0:T(512)S(1)}, bf16[512,256]{1,0:T(8,128)(2,1)}) fusion(f32[512]{0:T(512)S(1)} %bitcast.81, bf16[1,512,256]{2,1,0:T(8,128)(2,1)S(1)} %copy-done.2, f32[512]{0:T(512)S(1)} %bitcast.83, bf16[1,512,256]{2,1,0:T(8,128)(2,1)S(1)} %collective-permute-done.4, f32[512]{0:T(512)S(1)} %bitcast.85, ...), kind=kLoop, calls=%fused_computation.24 | loop fusion | flops 3275776 | bytes 1847300 | tf_op jit(solution)/shard_map/reduce_max | solution.py:24
  71.1 0.0 all-gather.2.cloned.1.call-update
  71.1 0.0 copy-start.4
  71.1 0.0 copy-start.5
  71.2 1.6 %divide_convert_fusion.3 = (bf16[1,512,256]{2,1,0:T(8,128)(2,1)}, f32[1,512,256]{2,1,0:T(8,128)}, bf16[1,512,256]{2,1,0:T(8,128)(2,1)}) fusion(f32[512]{0:T(512)S(1)} %get-tuple-element.22, bf16[1,512,256]{2,1,0:T(8,128)(2,1)S(1)} %copy-done.2, f32[512]{0:T(512)S(1)} %bitcast.82, f32[512]{0:T(512)S(1)} %bitcast.84, ...), kind=kLoop, calls=%fused_computation.23 | loop fusion | flops 3145728 | bytes 2633732 | tf_op jit(solution)/shard_map/convert_element_type | solution.py:25
  72.8 48.4 %all-gather.2.cloned.1.call-done = bf16[4096,256]{1,0:T(8,128)(2,1)} async-done(((bf16[512,256]{1,0:T(8,128)(2,1)}), bf16[4096,256]{1,0:T(8,128)(2,1)}) %all-gather.2.cloned.1.call-update) | async-done | bytes 2097168 | tf_op jit(solution)/shard_map/all_gather | solution.py:65
  121.2 3.0 %copy.27 = bf16[1,4096,256]{2,1,0:T(8,128)(2,1)} copy(bf16[1,4096,256]{2,1,0:T(8,128)(2,1)} %bitcast.74) | data formatting | bytes 4194304
  124.2 0.0 copy-done.4
  124.2 0.0 copy-done.5
  (21 shorter events, 0.2 us)
Async XLA Ops:
  7.2 114.0 %all-gather.2.cloned.1.call-start = ((), (), s32[]{:S(2)}) async-start(), calls=%async_computation | async-start | bytes 2359296 | tf_op jit(solution)/shard_map/all_gather | solution.py:65
  12.5 26.4 %collective-permute-start = (bf16[4,512,256]{2,1,0:T(8,128)(2,1)}, bf16[4,512,256]{2,1,0:T(8,128)(2,1)S(1)}, u32[]{:S(2)}, u32[]{:S(2)}) collective-permute-start(bf16[4,512,256]{2,1,0:T(8,128)(2,1)} %dynamic-slice_bitcast_fusion), channel_id=1, source_target_pairs={{0,4},{4,0},{8,12},{12,8},{16,20},{20,16},{24,28},{28,24},{1,5},{5... | collective-permute-start | bytes 3145736 | tf_op jit(solution)/shard_map/ppermute | solution.py:10
  15.5 23.4 %collective-permute-start.1 = (bf16[4,512]{1,0:T(4,128)(2,1)S(1)}, bf16[4,512]{1,0:T(4,128)(2,1)S(1)}, u32[]{:S(2)}, u32[]{:S(2)}) collective-permute-start(bf16[4,512]{1,0:T(4,128)(2,1)S(1)} %bitcast.89), channel_id=1, source_target_pairs={{0,4},{4,0},{8,12},{12,8},{16,20},{20,16},{24,28},{28,24},{1,5},{5... | collective-permute-start | bytes 12296 | tf_op jit(solution)/shard_map/ppermute | solution.py:10
  38.9 1.1 copy-start
  40.0 4.4 %copy-start.6 = (f32[1,512]{1,0:T(1,128)S(1)}, f32[1,512]{1,0:T(1,128)}, u32[]{:S(2)}) copy-start(f32[1,512]{1,0:T(1,128)} %param.9) | copy-start | bytes 6148
  42.1 17.4 %copy-start.7 = (f32[1,512]{1,0:T(1,128)S(1)}, f32[1,512]{1,0:T(1,128)}, u32[]{:S(2)}) copy-start(f32[1,512]{1,0:T(1,128)} %param.11) | copy-start | bytes 6148
  42.1 27.6 %copy-start.1 = (f32[1,512,256]{2,1,0:T(8,128)S(1)}, f32[1,512,256]{2,1,0:T(8,128)}, u32[]{:S(2)}) copy-start(f32[1,512,256]{2,1,0:T(8,128)} %param.7) | copy-start | bytes 1572868
  42.1 27.6 %copy-start.2 = (bf16[1,512,256]{2,1,0:T(8,128)(2,1)S(1)}, bf16[1,512,256]{2,1,0:T(8,128)(2,1)}, u32[]{:S(2)}) copy-start(bf16[1,512,256]{2,1,0:T(8,128)(2,1)} %param.10) | copy-start | bytes 786436
  42.1 27.6 %copy-start.3 = (bf16[1,512,256]{2,1,0:T(8,128)(2,1)S(1)}, bf16[1,512,256]{2,1,0:T(8,128)(2,1)}, u32[]{:S(2)}) copy-start(bf16[1,512,256]{2,1,0:T(8,128)(2,1)} %param.8) | copy-start | bytes 786436
  42.2 13.2 %collective-permute-start.2 = (bf16[2,512,256]{2,1,0:T(8,128)(2,1)S(1)}, bf16[2,512,256]{2,1,0:T(8,128)(2,1)S(1)}, u32[]{:S(2)}, u32[]{:S(2)}) collective-permute-start(bf16[2,512,256]{2,1,0:T(8,128)(2,1)S(1)} %dynamic-slice_bitcast_fusion.1), channel_id=1, source_target_pairs={{0,8},{4,12},{8,0},{12,4},{16,24},{20,28},{24,16},{28,20},{1,9},{5... | collective-permute-start | bytes 1572872 | tf_op jit(solution)/shard_map/ppermute | solution.py:10
  44.1 11.3 %collective-permute-start.3 = (bf16[2,512]{1,0:T(2,128)(2,1)S(1)}, bf16[2,512]{1,0:T(2,128)(2,1)S(1)}, u32[]{:S(2)}, u32[]{:S(2)}) collective-permute-start(bf16[2,512]{1,0:T(2,128)(2,1)S(1)} %bitcast.90), channel_id=1, source_target_pairs={{0,8},{4,12},{8,0},{12,4},{16,24},{20,28},{24,16},{28,20},{1,9},{5... | collective-permute-start | bytes 6152 | tf_op jit(solution)/shard_map/ppermute | solution.py:10
  56.4 13.3 %collective-permute-start.4 = (bf16[1,512,256]{2,1,0:T(8,128)(2,1)S(1)}, bf16[1,512,256]{2,1,0:T(8,128)(2,1)S(1)}, u32[]{:S(2)}, u32[]{:S(2)}) collective-permute-start(bf16[1,512,256]{2,1,0:T(8,128)(2,1)S(1)} %constant_dynamic-slice_fusion.1), channel_id=1, source_target_pairs={{0,16},{4,20},{8,24},{12,28},{16,0},{20,4},{24,8},{28,12},{1,17},{... | collective-permute-start | bytes 786440 | tf_op jit(solution)/shard_map/ppermute | solution.py:10
  59.1 10.6 %collective-permute-start.5 = (bf16[1,512]{1,0:T(2,128)(2,1)S(1)}, bf16[1,512]{1,0:T(2,128)(2,1)S(1)}, u32[]{:S(2)}, u32[]{:S(2)}) collective-permute-start(bf16[1,512]{1,0:T(2,128)(2,1)S(1)} %get-tuple-element.21), channel_id=1, source_target_pairs={{0,16},{4,20},{8,24},{12,28},{16,0},{20,4},{24,8},{28,12},{1,17},{... | collective-permute-start | bytes 3080 | tf_op jit(solution)/shard_map/ppermute | solution.py:10
  71.1 53.1 %copy-start.4 = (f32[512]{0:T(512)}, f32[512]{0:T(512)S(1)}, u32[]{:S(2)}) copy-start(f32[512]{0:T(512)S(1)} %get-tuple-element.22) | copy-start | bytes 6148
  71.1 53.1 %copy-start.5 = (f32[512]{0:T(512)}, f32[512]{0:T(512)S(1)}, u32[]{:S(2)}) copy-start(f32[512]{0:T(512)S(1)} %get-tuple-element.23) | copy-start | bytes 6148
Sparse Core Ops, SparseCore 0:
  71.2 49.8 all-gather.1
where the time goes:
time: 131 us
  waiting for transfers between devices  92.9 us (71%)
  between operations  14.3 us (11%)
  other arithmetic  11.3 us (9%)
  starting transfers between devices  8.29 us (6%)
  local copies, waits for them, and re-layouts  4.25 us (3%)
    all_gather x1, waiting for transfers between devices, per_device(): lax.all_gather(master_new.astype(jnp.bfloat16), 'dp', axis=0, tiled=True)  48.4 us
    ppermute x6, waiting for transfers between devices, partner(): lax.ppermute(shard, axis, [(i, i ^ 1 << apart) for i in range(lax.axis_si...  44.5 us
    ppermute x6, starting transfers between devices, partner(): lax.ppermute(shard, axis, [(i, i ^ 1 << apart) for i in range(lax.axis_si...  8.25 us
    convert_element_type x3, other arithmetic, block_code(): (values / scale.astype(jnp.float32)[..., None]).astype(jnp.bfloat16)  4.47 us
    reduce_max x3, other arithmetic, block_code(): scale = (jnp.max(jnp.abs(values), axis=-1) + 1e-06).astype(jnp.bfloat16)  3.77 us
    unnamed x21, local copies, waits for them, and re-layouts  3.11 us
  transfers between devices with their start and end apart: 7, of which 4 were waited for; matrix products, arithmetic and copies ran while one was open for 1% of the time, Pallas kernels for 0%

commit v1 on v0

v1 whole, which is shorter than its diff:
```python
import functools

import jax
import jax.numpy as jnp
from jax import lax
from jax.experimental import pallas as pl
from jax.experimental.pallas import tpu as pltpu
from jax.sharding import PartitionSpec as P

STEP = 8
ROWS = 128
MESH = pl.DeviceIdType.MESH


def spread(row):
    return jnp.transpose(jnp.broadcast_to(row, (ROWS, ROWS)))


def gather_row(column):
    return jnp.transpose(jnp.broadcast_to(column, (ROWS, ROWS)))[0:1, :]


def kernel(
    outer, grads, master, m_codes, m_scale, v_codes, v_scale,
    master_out, m_out, ms_out, v_out, vs_out, weights,
    own, xgot, stage, mine, zgot, wbuf,
    master_in, m_in, v_in, ms_in, vs_in, master_new, m_new, v_new, ms_new, vs_new,
    own_sem, state_sem, out_sem, wout_sem,
    xs_send, xs_recv, zs_send, zs_recv, zg_send, zg_recv, xg_send, xg_recv,
):
    owned, width = master.shape[1], master.shape[2]
    pieces = owned // ROWS
    replicas = 2 * outer
    me = lax.axis_index("dp")
    x = lax.rem(me, 2)
    z = lax.div(me, 2)
    other = z * 2 + 1 - x

    def ahead(step):
        return lax.rem(z + 1 + step, outer)

    def behind(step):
        return lax.rem(z + 2 * outer - 1 - step, outer)

    def rows_of(owner, piece):
        return pl.ds(pl.multiple_of(owner * owned + piece * ROWS, ROWS), ROWS)

    def remote(src, dst, send, recv, device):
        return pltpu.make_async_remote_copy(
            src_ref=src, dst_ref=dst, send_sem=send, recv_sem=recv,
            device_id={"dp": device}, device_id_type=MESH,
        )

    barrier = pltpu.get_barrier_semaphore()
    pl.semaphore_signal(barrier, inc=1, device_id={"dp": other}, device_id_type=MESH)
    for step in range(outer - 1):
        pl.semaphore_signal(
            barrier, inc=1, device_id={"dp": ahead(step) * 2 + x}, device_id_type=MESH
        )

    own_copies = {}
    for k in range(pieces):
        for step in range(outer):
            copy = pltpu.make_async_copy(
                grads.at[0, 0, rows_of(ahead(step) * 2 + x, k), :],
                own.at[k, step], own_sem.at[k, step],
            )
            copy.start()
            own_copies[k, step] = copy
    state_copies = []
    for i, (src, dst) in enumerate((
        (master, master_in), (m_codes, m_in), (v_codes, v_in), (m_scale, ms_in), (v_scale, vs_in),
    )):
        copy = pltpu.make_async_copy(src, dst, state_sem.at[i])
        copy.start()
        state_copies.append(copy)

    pl.semaphore_wait(barrier, outer)
    xs = {}
    for k in range(pieces):
        for step in range(outer):
            copy = remote(
                grads.at[0, 0, rows_of(ahead(step) * 2 + 1 - x, k), :], xgot.at[k, step],
                xs_send.at[k, step], xs_recv.at[k, step], other,
            )
            copy.start()
            xs[k, step] = copy

    zs, zg, xg, locals_ = {}, {}, {}, []

    def pair_sums(k):
        for step in range(outer):
            own_copies[k, step].wait()
            xs[k, step].wait_recv()
            total = own[k, step].astype(jnp.float32) + xgot[k, step].astype(jnp.float32)
            if step == outer - 1:
                mine[k] = total
            else:
                stage[k, step] = total.astype(jnp.bfloat16)
                copy = remote(
                    stage.at[k, step], zgot.at[k, step],
                    zs_send.at[k, step], zs_recv.at[k, step], ahead(step) * 2 + x,
                )
                copy.start()
                zs[k, step] = copy

    def update(k):
        if k == 0:
            for copy in state_copies:
                copy.wait()
        rows = pl.ds(k * ROWS, ROWS)
        total = mine[k]
        for step in range(outer - 1):
            zs[k, step].wait_recv()
            total = total + zgot[k, step].astype(jnp.float32)
        mean = total * (1.0 / replicas)
        ms = spread(ms_in[0:1, rows])
        vs = spread(vs_in[0:1, rows])
        ms = jnp.concatenate([ms] * (width // ROWS), axis=1)
        vs = jnp.concatenate([vs] * (width // ROWS), axis=1)
        one = 0.9 * m_in[0, rows].astype(jnp.float32) * ms + 0.1 * mean
        two = 0.95 * v_in[0, rows].astype(jnp.float32) * vs + 0.05 * mean * mean
        first_fix = 1.0 - 0.9**STEP
        second_fix = 1.0 - 0.95**STEP
        new = master_in[0, rows] - (0.1 / first_fix) * one / (
            jnp.sqrt(two * (1.0 / second_fix)) + 1e-08
        )
        wbuf[z, rows] = new.astype(jnp.bfloat16)
        for step in range(outer - 1):
            copy = remote(
                wbuf.at[z, rows], wbuf.at[z, rows],
                zg_send.at[k, step], zg_recv.at[k, step], ahead(step) * 2 + x,
            )
            copy.start()
            zg[k, step] = copy
        pass_on(k, outer - 1, z)
        master_new[0, rows] = new
        one_top = jnp.max(jnp.abs(one), axis=-1, keepdims=True) + 1e-06
        two_top = jnp.max(jnp.abs(two), axis=-1, keepdims=True) + 1e-06
        m_new[0, rows] = (one / one_top).astype(jnp.bfloat16)
        v_new[0, rows] = (two / two_top).astype(jnp.bfloat16)
        ms_new[0:1, rows] = gather_row(one_top)
        vs_new[0:1, rows] = gather_row(two_top)
        for i, (src, dst) in enumerate((
            (master_new, master_out), (m_new, m_out), (v_new, v_out),
        )):
            copy = pltpu.make_async_copy(src.at[0, rows], dst.at[0, rows], out_sem.at[k, i])
            copy.start()
            locals_.append(copy)

    def pass_on(k, step, source):
        rows = pl.ds(k * ROWS, ROWS)
        target = weights.at[0, rows_of(source * 2 + x, k), :]
        copy = remote(
            wbuf.at[source, rows], target, xg_send.at[k, step], xg_recv.at[k, step], other
        )
        copy.start()
        xg[k, step] = copy
        local = pltpu.make_async_copy(wbuf.at[source, rows], target, wout_sem.at[k, step])
        local.start()
        locals_.append(local)

    def forward(k):
        for step in range(outer - 1):
            zg[k, step].wait_recv()
            pass_on(k, step, behind(step))

    for tick in range(pieces + 2):
        if tick < pieces:
            pair_sums(tick)
        if 0 <= tick - 1 < pieces:
            update(tick - 1)
            if tick == pieces:
                for i, (src, dst) in enumerate(((ms_new, ms_out), (vs_new, vs_out))):
                    copy = pltpu.make_async_copy(src, dst, state_sem.at[i])
                    copy.start()
                    locals_.append(copy)
        if 0 <= tick - 2 < pieces:
            forward(tick - 2)

    for group in (xs, zs, zg, xg):
        for copy in group.values():
            copy.wait_send()
    for copy in xg.values():
        copy.wait_recv()
    for copy in locals_:
        copy.wait()


def per_device(grads, master, m_codes, m_scale, v_codes, v_scale):
    outer = lax.axis_size("dp") // 2
    _, owned, width = master.shape
    pieces = owned // ROWS
    bf16, f32 = jnp.bfloat16, jnp.float32
    dma = pltpu.SemaphoreType.DMA
    shape = jax.ShapeDtypeStruct
    state = (1, owned, width)
    outs = pl.pallas_call(
        functools.partial(kernel, outer),
        out_shape=(
            shape(state, f32), shape(state, bf16), shape((1, owned), f32),
            shape(state, bf16), shape((1, owned), f32),
            shape((1, 2 * outer * owned, width), bf16),
        ),
        in_specs=[pl.BlockSpec(memory_space=pl.ANY)] * 6,
        out_specs=[pl.BlockSpec(memory_space=pl.ANY)] * 6,
        scratch_shapes=[
            pltpu.VMEM((pieces, outer, ROWS, width), bf16),
            pltpu.VMEM((pieces, outer, ROWS, width), bf16),
            pltpu.VMEM((pieces, outer - 1, ROWS, width), bf16),
            pltpu.VMEM((pieces, ROWS, width), f32),
            pltpu.VMEM((pieces, outer - 1, ROWS, width), bf16),
            pltpu.VMEM((outer, owned, width), bf16),
            pltpu.VMEM(state, f32), pltpu.VMEM(state, bf16), pltpu.VMEM(state, bf16),
            pltpu.VMEM((1, owned), f32), pltpu.VMEM((1, owned), f32),
            pltpu.VMEM(state, f32), pltpu.VMEM(state, bf16), pltpu.VMEM(state, bf16),
            pltpu.VMEM((1, owned), f32), pltpu.VMEM((1, owned), f32),
            dma((pieces, outer)), dma((5,)), dma((pieces, 3)), dma((pieces, outer)),
            dma((pieces, outer)), dma((pieces, outer)),
            dma((pieces, outer - 1)), dma((pieces, outer - 1)),
            dma((pieces, outer - 1)), dma((pieces, outer - 1)),
            dma((pieces, outer)), dma((pieces, outer)),
        ],
        compiler_params=pltpu.CompilerParams(collective_id=0, has_side_effects=True),
    )(grads, master, m_codes, m_scale, v_codes, v_scale)
    return tuple(outs)


def solution(mesh):
    return jax.shard_map(
        per_device,
        mesh=mesh,
        in_specs=(
            P("dp", "mp", None, None),
            P("mp", "dp", None),
            P("mp", "dp", None),
            P("mp", "dp"),
            P("mp", "dp", None),
            P("mp", "dp"),
        ),
        out_specs=(
            P("mp", "dp", None),
            P("mp", "dp", None),
            P("mp", "dp"),
            P("mp", "dp", None),
            P("mp", "dp"),
            P("mp", None, None),
        ),
        check_vma=False,
    )
```

time: 131 us -> 69 us (0.53)
  waiting for transfers between devices: 92.9 us -> 0 us
  Pallas kernels: 0 us -> 59.6 us
  between operations: 14.3 us -> 0.66 us
  other arithmetic: 11.3 us -> 0 us
  starting transfers between devices: 8.29 us -> 0 us
  local copies, waits for them, and re-layouts: 4.25 us -> 8.52 us
    pallas_call x0 -> x1, Pallas kernels: none -> 59.6 us  [per_device(): pl.pallas_call(functools.partial(kernel, outer), out_shape=(shape(state,...]
    all_gather x1 -> x0, waiting for transfers between devices: 48.4 us -> none  [per_device(): lax.all_gather(master_new.astype(jnp.bfloat16), 'dp', axis=0, tiled=True)]
    ppermute x6 -> x0, waiting for transfers between devices: 44.5 us -> none  [partner(): lax.ppermute(shard, axis, [(i, i ^ 1 << apart) for i in range(lax.axis_si...]
    ppermute x6 -> x0, starting transfers between devices: 8.25 us -> none  [partner(): lax.ppermute(shard, axis, [(i, i ^ 1 << apart) for i in range(lax.axis_si...]
    convert_element_type x13 -> x0, other arithmetic: 6.15 us -> none  [the longest x3 4.47 us: block_code(): (values / scale.astype(jnp.float32)[..., None]).astype(jnp.bfloat16)]
    unnamed x21 -> x10, local copies, waits for them, and re-layouts: 3.11 us -> 8.52 us
    reduce_max x4 -> x0, other arithmetic: 5.13 us -> none  [the longest x3 3.77 us: block_code(): scale = (jnp.max(jnp.abs(values), axis=-1) + 1e-06).astype(jnp.bfloat16)]
  transfers between devices with their start and end apart: 7 -> 0, of which waited for: 4 -> 0; matrix products, arithmetic and copies ran while one was open for 1% -> 0% of each run, Pallas kernels for 0% -> 0%
where the time goes in v1:
time: 69 us; the launch traced here: 68.7 us
  Pallas kernels  59.6 us (86%)
  local copies, waits for them, and re-layouts  8.52 us (12%)
    pallas_call x1, Pallas kernels, per_device(): pl.pallas_call(functools.partial(kernel, outer), out_shape=(shape(state,...  59.6 us
    unnamed x10, local copies, waits for them, and re-layouts  8.52 us

profile of v1, /device:TPU:0, one launch (start us, length us, event | category | flops | bytes accessed | tf_op | source)
XLA Modules:
  0.0 68.7 jit_solution(4445188939703474997)
XLA Ops:
  0.6 59.6 %shard_map.109 = (f32[1,512,256]{2,1,0:T(8,128)}, bf16[1,512,256]{2,1,0:T(8,128)(2,1)}, f32[1,512]{1,0:T(1,128)}, bf16[1,512,256]{2,1,0:T(8,128)(2,1)}, f32[1,512]{1,0:T(1,128)}, /*index=5*/bf16[1,4096,256]{2,1,0:T(8,128)(2,1)}) custom-call(bf16[1,1,4096,256]{3,2,1,0:T(8,128)(2,1)} %grads.1, f32[1,512,256]{2,1,0:T(8,128)} %master.1, ...), custom_call_target="tpu_custom_call" | custom-call | tf_op jit(solution)/shard_map/pallas_call | solution.py:198
  60.2 0.0 copy-start.1
  60.2 0.0 copy-start
  60.2 2.0 %copy.18 = f32[1,512,256]{2,1,0:T(8,128)} copy(f32[1,512,256]{2,1,0:T(8,128)} %get-tuple-element.12) | data formatting | bytes 1048576
  62.2 1.7 %copy.19 = bf16[1,512,256]{2,1,0:T(8,128)(2,1)} copy(bf16[1,512,256]{2,1,0:T(8,128)(2,1)} %get-tuple-element.13) | data formatting | bytes 524288
  63.9 1.3 %copy.20 = f32[1,512]{1,0:T(1,128)} copy(f32[1,512]{1,0:T(1,128)} %get-tuple-element.14) | data formatting | bytes 4096
  65.2 1.7 %copy.21 = bf16[1,512,256]{2,1,0:T(8,128)(2,1)} copy(bf16[1,512,256]{2,1,0:T(8,128)(2,1)} %get-tuple-element.15) | data formatting | bytes 524288
  66.8 0.0 copy-done.1
  66.8 0.6 copy.22
  67.4 0.0 copy-done
  67.4 1.3 %copy.23 = bf16[1,4096,256]{2,1,0:T(8,128)(2,1)} copy(bf16[1,4096,256]{2,1,0:T(8,128)(2,1)S(1)} %copy-done) | data formatting | bytes 4194304
Async XLA Ops:
  60.2 6.6 %copy-start.1 = (f32[1,512]{1,0:T(1,128)S(1)}, f32[1,512]{1,0:T(1,128)}, u32[]{:S(2)}) copy-start(f32[1,512]{1,0:T(1,128)} %get-tuple-element.16) | copy-start | bytes 6148
  60.2 7.2 %copy-start = (bf16[1,4096,256]{2,1,0:T(8,128)(2,1)S(1)}, bf16[1,4096,256]{2,1,0:T(8,128)(2,1)}, u32[]{:S(2)}) copy-start(bf16[1,4096,256]{2,1,0:T(8,128)(2,1)} %get-tuple-element.17) | copy-start | bytes 6291460

commit v2 on v1

--- a/solution.py
+++ b/solution.py
@@ -1,4 +1,5 @@
 import functools
+import math
 
 import jax
 import jax.numpy as jnp
@@ -9,6 +10,8 @@
 
 STEP = 8
 ROWS = 128
+VMEM_ALL = 67043328
+VMEM_GRANT = 60 * 1024 * 1024
 MESH = pl.DeviceIdType.MESH
 
 
@@ -22,11 +25,11 @@
 
 def kernel(
     outer, grads, master, m_codes, m_scale, v_codes, v_scale,
-    master_out, m_out, ms_out, v_out, vs_out, weights,
-    own, xgot, stage, mine, zgot, wbuf,
-    master_in, m_in, v_in, ms_in, vs_in, master_new, m_new, v_new, ms_new, vs_new,
-    own_sem, state_sem, out_sem, wout_sem,
-    xs_send, xs_recv, zs_send, zs_recv, zg_send, zg_recv, xg_send, xg_recv,
+    master_new, m_new, ms_new, v_new, vs_new, weights,
+    own, xgot, stage, mine, zgot,
+    master_in, m_in, v_in, ms_in, vs_in,
+    own_sem, state_sem,
+    xs_send, xs_recv, zs_send, zs_recv, right_send, left_send, zg_recv, xg_send, xg_recv,
 ):
     owned, width = master.shape[1], master.shape[2]
     pieces = owned // ROWS
@@ -38,9 +41,6 @@
 
     def ahead(step):
         return lax.rem(z + 1 + step, outer)
-
-    def behind(step):
-        return lax.rem(z + 2 * outer - 1 - step, outer)
 
     def rows_of(owner, piece):
         return pl.ds(pl.multiple_of(owner * owned + piece * ROWS, ROWS), ROWS)
@@ -86,7 +86,7 @@
             copy.start()
             xs[k, step] = copy
 
-    zs, zg, xg, locals_ = {}, {}, {}, []
+    zs = {}
 
     def pair_sums(k):
         for step in range(outer):
@@ -103,6 +103,27 @@
                 )
                 copy.start()
                 zs[k, step] = copy
+
+    def weight_rows(k, source):
+        return weights.at[0, rows_of(source * 2 + x, k), :]
+
+    def rightward(k, source):
+        rows = weight_rows(k, source)
+        return remote(
+            rows, rows, right_send.at[k, source], zg_recv.at[k, source],
+            lax.min(z + 1, outer - 1) * 2 + x,
+        )
+
+    def leftward(k, source):
+        rows = weight_rows(k, source)
+        return remote(
+            rows, rows, left_send.at[k, source], zg_recv.at[k, source],
+            lax.max(z - 1, 0) * 2 + x,
+        )
+
+    def across(k, source):
+        rows = weight_rows(k, source)
+        return remote(rows, rows, xg_send.at[k, source], xg_recv.at[k, source], other)
 
     def update(k):
         if k == 0:
@@ -125,15 +146,10 @@
         new = master_in[0, rows] - (0.1 / first_fix) * one / (
             jnp.sqrt(two * (1.0 / second_fix)) + 1e-08
         )
-        wbuf[z, rows] = new.astype(jnp.bfloat16)
-        for step in range(outer - 1):
-            copy = remote(
-                wbuf.at[z, rows], wbuf.at[z, rows],
-                zg_send.at[k, step], zg_recv.at[k, step], ahead(step) * 2 + x,
-            )
-            copy.start()
-            zg[k, step] = copy
-        pass_on(k, outer - 1, z)
+        weights[0, rows_of(me, k), :] = new.astype(jnp.bfloat16)
+        pl.when(z < outer - 1)(lambda: rightward(k, z).start())
+        pl.when(z > 0)(lambda: leftward(k, z).start())
+        across(k, z).start()
         master_new[0, rows] = new
         one_top = jnp.max(jnp.abs(one), axis=-1, keepdims=True) + 1e-06
         two_top = jnp.max(jnp.abs(two), axis=-1, keepdims=True) + 1e-06
@@ -141,49 +157,53 @@
         v_new[0, rows] = (two / two_top).astype(jnp.bfloat16)
         ms_new[0:1, rows] = gather_row(one_top)
         vs_new[0:1, rows] = gather_row(two_top)
-        for i, (src, dst) in enumerate((
-            (master_new, master_out), (m_new, m_out), (v_new, v_out),
-        )):
-            copy = pltpu.make_async_copy(src.at[0, rows], dst.at[0, rows], out_sem.at[k, i])
-            copy.start()
-            locals_.append(copy)
-
-    def pass_on(k, step, source):
-        rows = pl.ds(k * ROWS, ROWS)
-        target = weights.at[0, rows_of(source * 2 + x, k), :]
-        copy = remote(
-            wbuf.at[source, rows], target, xg_send.at[k, step], xg_recv.at[k, step], other
-        )
-        copy.start()
-        xg[k, step] = copy
-        local = pltpu.make_async_copy(wbuf.at[source, rows], target, wout_sem.at[k, step])
-        local.start()
-        locals_.append(local)
-
-    def forward(k):
-        for step in range(outer - 1):
-            zg[k, step].wait_recv()
-            pass_on(k, step, behind(step))
-
-    for tick in range(pieces + 2):
+
+    def forward(k, apart):
+        @pl.when(z >= apart)
+        def _():
+            source = z - apart
+            rightward(k, source).wait_recv()
+            pl.when(z < outer - 1)(lambda: rightward(k, source).start())
+            across(k, source).start()
+
+        @pl.when(z + apart < outer)
+        def _():
+            source = z + apart
+            leftward(k, source).wait_recv()
+            pl.when(z > 0)(lambda: leftward(k, source).start())
+            across(k, source).start()
+
+    for tick in range(pieces + outer):
         if tick < pieces:
             pair_sums(tick)
         if 0 <= tick - 1 < pieces:
             update(tick - 1)
-            if tick == pieces:
-                for i, (src, dst) in enumerate(((ms_new, ms_out), (vs_new, vs_out))):
-                    copy = pltpu.make_async_copy(src, dst, state_sem.at[i])
-                    copy.start()
-                    locals_.append(copy)
-        if 0 <= tick - 2 < pieces:
-            forward(tick - 2)
-
-    for group in (xs, zs, zg, xg):
+        for apart in range(1, outer):
+            if 0 <= tick - 1 - apart < pieces:
+                forward(tick - 1 - apart, apart)
+
+    for group in (xs, zs):
         for copy in group.values():
             copy.wait_send()
-    for copy in xg.values():
-        copy.wait_recv()
-    for copy in locals_:
+    for k in range(pieces):
+        for source in range(outer):
+            across(k, source).wait_send()
+            pl.when((source <= z) & (z < outer - 1))(lambda: rightward(k, source).wait_send())
+            pl.when((source >= z) & (z > 0))(lambda: leftward(k, source).wait_send())
+    for k in range(pieces):
+        for source in range(outer):
+            across(k, source).wait_recv()
+
+
+def write_out(*refs):
+    sem = refs[-1]
+    half = (len(refs) - 1) // 2
+    copies = [
+        pltpu.make_async_copy(refs[i], refs[half + i], sem.at[i]) for i in range(half)
+    ]
+    for copy in copies[::-1]:
+        copy.start()
+    for copy in copies:
         copy.wait()
 
 
@@ -195,35 +215,44 @@
     dma = pltpu.SemaphoreType.DMA
     shape = jax.ShapeDtypeStruct
     state = (1, owned, width)
+    out_shapes = (
+        (state, f32), (state, bf16), ((1, owned), f32),
+        (state, bf16), ((1, owned), f32),
+        ((1, 2 * outer * owned, width), bf16),
+    )
+    kept = sum(math.prod(dims) * jnp.dtype(kind).itemsize for dims, kind in out_shapes)
     outs = pl.pallas_call(
         functools.partial(kernel, outer),
-        out_shape=(
-            shape(state, f32), shape(state, bf16), shape((1, owned), f32),
-            shape(state, bf16), shape((1, owned), f32),
-            shape((1, 2 * outer * owned, width), bf16),
-        ),
-        in_specs=[pl.BlockSpec(memory_space=pl.ANY)] * 6,
-        out_specs=[pl.BlockSpec(memory_space=pl.ANY)] * 6,
+        out_shape=tuple(pltpu.VMEM(*each) for each in out_shapes),
+        in_specs=[pl.BlockSpec(memory_space=pltpu.HBM)] * 6,
+        out_specs=[pl.BlockSpec(memory_space=pltpu.VMEM)] * 6,
         scratch_shapes=[
             pltpu.VMEM((pieces, outer, ROWS, width), bf16),
             pltpu.VMEM((pieces, outer, ROWS, width), bf16),
             pltpu.VMEM((pieces, outer - 1, ROWS, width), bf16),
             pltpu.VMEM((pieces, ROWS, width), f32),
             pltpu.VMEM((pieces, outer - 1, ROWS, width), bf16),
-            pltpu.VMEM((outer, owned, width), bf16),
             pltpu.VMEM(state, f32), pltpu.VMEM(state, bf16), pltpu.VMEM(state, bf16),
             pltpu.VMEM((1, owned), f32), pltpu.VMEM((1, owned), f32),
-            pltpu.VMEM(state, f32), pltpu.VMEM(state, bf16), pltpu.VMEM(state, bf16),
-            pltpu.VMEM((1, owned), f32), pltpu.VMEM((1, owned), f32),
-            dma((pieces, outer)), dma((5,)), dma((pieces, 3)), dma((pieces, outer)),
+            dma((pieces, outer)), dma((5,)),
             dma((pieces, outer)), dma((pieces, outer)),
             dma((pieces, outer - 1)), dma((pieces, outer - 1)),
-            dma((pieces, outer - 1)), dma((pieces, outer - 1)),
+            dma((pieces, outer)), dma((pieces, outer)), dma((pieces, outer)),
             dma((pieces, outer)), dma((pieces, outer)),
         ],
-        compiler_params=pltpu.CompilerParams(collective_id=0, has_side_effects=True),
+        compiler_params=pltpu.CompilerParams(
+            collective_id=0, has_side_effects=True,
+            vmem_limit_bytes=min(VMEM_GRANT, VMEM_ALL - kept - 2**18),
+        ),
     )(grads, master, m_codes, m_scale, v_codes, v_scale)
-    return tuple(outs)
+    return tuple(pl.pallas_call(
+        write_out,
+        out_shape=tuple(shape(*each) for each in out_shapes),
+        in_specs=[pl.BlockSpec(memory_space=pltpu.VMEM)] * 6,
+        out_specs=[pl.BlockSpec(memory_space=pl.ANY)] * 6,
+        scratch_shapes=[dma((6,))],
+        compiler_params=pltpu.CompilerParams(vmem_limit_bytes=2**20),
+    )(*[pltpu.with_memory_space_constraint(o, pltpu.VMEM) for o in outs]))
 
 
 def solution(mesh):

time: 69 us -> 56.1 us (0.81)
  local copies, waits for them, and re-layouts: 8.52 us -> 0 us
  Pallas kernels: 59.6 us -> 55.3 us
    unnamed x10 -> x0, local copies, waits for them, and re-layouts: 8.52 us -> none
    pallas_call x1 -> x2, Pallas kernels: 59.6 us -> 55.3 us  [the longest x1 53.6 us: per_device(): pl.pallas_call(functools.partial(kernel, outer), out_shape=tuple((pltpu.V...]
where the time goes in v2:
time: 56.1 us; the launch traced here: 55.9 us
  Pallas kernels  55.3 us (99%)
  between operations  0.64 us (1%)
    pallas_call x1, Pallas kernels, per_device(): pl.pallas_call(functools.partial(kernel, outer), out_shape=tuple((pltpu.V...  53.6 us
    pallas_call x1, Pallas kernels, per_device(): pl.pallas_call(write_out, out_shape=tuple((shape(*each) for each in out_s...  1.73 us

profile of v2, /device:TPU:0, one launch (start us, length us, event | category | flops | bytes accessed | tf_op | source)
XLA Modules:
  0.0 55.9 jit_solution(7741429225865956322)
XLA Ops:
  0.6 53.6 %shard_map.109 = (f32[1,512,256]{2,1,0:T(8,128)S(1)}, bf16[1,512,256]{2,1,0:T(8,128)(2,1)S(1)}, f32[1,512]{1,0:T(1,128)S(1)}, bf16[1,512,256]{2,1,0:T(8,128)(2,1...) custom-call(bf16[1,1,4096,256]{3,2,1,0:T(8,128)(2,1)} %grads.1, f32[1,512,256]{2,1,0:T(8,128)} %master.1, ...), custom_call_target="tpu_custom_call" | custom-call | tf_op jit(solution)/shard_map/pallas_call | solution.py:224
  54.2 1.7 %shard_map.110 = (f32[1,512,256]{2,1,0:T(8,128)}, bf16[1,512,256]{2,1,0:T(8,128)(2,1)}, f32[1,512]{1,0:T(1,128)}, bf16[1,512,256]{2,1,0:T(8,128)(2,1)}, f32[1,512]{1,0:T(1,128)}, /*index=5*/bf16[1,4096,256]{2,1,0:T(8,128)(2,1)}) custom-call(f32[1,512,256]{2,1,0:T(8,128)S(1)} %get-tuple-element.12.refs_0_, ...), custom_call_target="tpu_custom_call" | custom-call | tf_op jit(solution)/shard_map/pallas_call | solution.py:248

commit v3 on v2

--- a/solution.py
+++ b/solution.py
@@ -26,10 +26,11 @@
 def kernel(
     outer, grads, master, m_codes, m_scale, v_codes, v_scale,
     master_new, m_new, ms_new, v_new, vs_new, weights,
-    own, xgot, stage, mine, zgot,
+    own, xgot, stage, mine, pgot, zgot,
     master_in, m_in, v_in, ms_in, vs_in,
     own_sem, state_sem,
-    xs_send, xs_recv, zs_send, zs_recv, right_send, left_send, zg_recv, xg_send, xg_recv,
+    xs_send, xs_recv, zs_send, pair_recv, zs_recv,
+    right_send, left_send, zg_recv, xg_send, xg_recv,
 ):
     owned, width = master.shape[1], master.shape[2]
     pieces = owned // ROWS
@@ -38,6 +39,13 @@
     x = lax.rem(me, 2)
     z = lax.div(me, 2)
     other = z * 2 + 1 - x
+    odd = lax.rem(z, 2)
+    pair = z + 1 - 2 * odd
+    given = z * odd + (outer - 1 - z) * (1 - odd)
+    x_first = pieces // 2
+
+    def target(step):
+        return step * odd + (outer - 1 - step) * (1 - odd)
 
     def ahead(step):
         return lax.rem(z + 1 + step, outer)
@@ -62,7 +70,7 @@
     for k in range(pieces):
         for step in range(outer):
             copy = pltpu.make_async_copy(
-                grads.at[0, 0, rows_of(ahead(step) * 2 + x, k), :],
+                grads.at[0, 0, rows_of(target(step) * 2 + x, k), :],
                 own.at[k, step], own_sem.at[k, step],
             )
             copy.start()
@@ -77,53 +85,79 @@
 
     pl.semaphore_wait(barrier, outer)
     xs = {}
-    for k in range(pieces):
+
+    def send_pairs(k):
         for step in range(outer):
             copy = remote(
-                grads.at[0, 0, rows_of(ahead(step) * 2 + 1 - x, k), :], xgot.at[k, step],
+                grads.at[0, 0, rows_of(target(step) * 2 + 1 - x, k), :], xgot.at[k, step],
                 xs_send.at[k, step], xs_recv.at[k, step], other,
             )
             copy.start()
             xs[k, step] = copy
 
-    zs = {}
+    def to_pair(k, step):
+        return remote(
+            stage.at[k, step], pgot.at[k, target(step)],
+            zs_send.at[k, step], pair_recv.at[k, target(step)], pair * 2 + x,
+        )
+
+    def to_owner(k, step, slot):
+        return remote(
+            stage.at[k, step], zgot.at[k, slot],
+            zs_send.at[k, step], zs_recv.at[k, slot], target(step) * 2 + x,
+        )
+
+    def pair_sum(k, step):
+        return own[k, step].astype(jnp.float32) + xgot[k, step].astype(jnp.float32)
 
     def pair_sums(k):
         for step in range(outer):
             own_copies[k, step].wait()
             xs[k, step].wait_recv()
-            total = own[k, step].astype(jnp.float32) + xgot[k, step].astype(jnp.float32)
-            if step == outer - 1:
-                mine[k] = total
-            else:
+
+            @pl.when(step < given)
+            def _():
+                stage[k, step] = pair_sum(k, step).astype(jnp.bfloat16)
+                to_pair(k, step).start()
+
+            @pl.when(step == given)
+            def _():
+                mine[k] = pair_sum(k, step)
+
+    def merges(k):
+        for step in range(1, outer):
+
+            @pl.when(step > given)
+            def _():
+                to_pair(k, step).wait_recv()
+                total = pair_sum(k, step) + pgot[k, target(step)].astype(jnp.float32)
                 stage[k, step] = total.astype(jnp.bfloat16)
-                copy = remote(
-                    stage.at[k, step], zgot.at[k, step],
-                    zs_send.at[k, step], zs_recv.at[k, step], ahead(step) * 2 + x,
-                )
-                copy.start()
-                zs[k, step] = copy
-
-    def weight_rows(k, source):
-        return weights.at[0, rows_of(source * 2 + x, k), :]
-
-    def rightward(k, source):
-        rows = weight_rows(k, source)
+                to_owner(k, step, lax.div(z, 2)).start()
+
+    def weight_rows(k, chunk):
+        return weights.at[0, rows_of(chunk, k), :]
+
+    def rightward(k, chunk):
+        rows = weight_rows(k, chunk)
         return remote(
-            rows, rows, right_send.at[k, source], zg_recv.at[k, source],
+            rows, rows, right_send.at[k, chunk], zg_recv.at[k, chunk],
             lax.min(z + 1, outer - 1) * 2 + x,
         )
 
-    def leftward(k, source):
-        rows = weight_rows(k, source)
+    def leftward(k, chunk):
+        rows = weight_rows(k, chunk)
         return remote(
-            rows, rows, left_send.at[k, source], zg_recv.at[k, source],
+            rows, rows, left_send.at[k, chunk], zg_recv.at[k, chunk],
             lax.max(z - 1, 0) * 2 + x,
         )
 
     def across(k, source):
-        rows = weight_rows(k, source)
+        rows = weight_rows(k, source * 2 + x)
         return remote(rows, rows, xg_send.at[k, source], xg_recv.at[k, source], other)
+
+    def both_ways(k, chunk):
+        pl.when(z < outer - 1)(lambda: rightward(k, chunk).start())
+        pl.when(z > 0)(lambda: leftward(k, chunk).start())
 
     def update(k):
         if k == 0:
@@ -131,9 +165,14 @@
                 copy.wait()
         rows = pl.ds(k * ROWS, ROWS)
         total = mine[k]
-        for step in range(outer - 1):
-            zs[k, step].wait_recv()
-            total = total + zgot[k, step].astype(jnp.float32)
+        remote(
+            stage.at[k, 0], pgot.at[k, z], zs_send.at[k, 0], pair_recv.at[k, z], pair * 2 + x
+        ).wait_recv()
+        total = total + pgot[k, z].astype(jnp.float32)
+        for i in range(outer // 2 - 1):
+            slot = lax.rem(lax.div(z, 2) + 1 + i, outer // 2)
+            to_owner(k, 0, slot).wait_recv()
+            total = total + zgot[k, slot].astype(jnp.float32)
         mean = total * (1.0 / replicas)
         ms = spread(ms_in[0:1, rows])
         vs = spread(vs_in[0:1, rows])
@@ -147,9 +186,12 @@
             jnp.sqrt(two * (1.0 / second_fix)) + 1e-08
         )
         weights[0, rows_of(me, k), :] = new.astype(jnp.bfloat16)
-        pl.when(z < outer - 1)(lambda: rightward(k, z).start())
-        pl.when(z > 0)(lambda: leftward(k, z).start())
-        across(k, z).start()
+        if k < x_first:
+            across(k, z).start()
+            both_ways(k, me)
+        else:
+            both_ways(k, me)
+            across(k, z).start()
         master_new[0, rows] = new
         one_top = jnp.max(jnp.abs(one), axis=-1, keepdims=True) + 1e-06
         two_top = jnp.max(jnp.abs(two), axis=-1, keepdims=True) + 1e-06
@@ -158,39 +200,59 @@
         ms_new[0:1, rows] = gather_row(one_top)
         vs_new[0:1, rows] = gather_row(two_top)
 
-    def forward(k, apart):
+    def from_partner(k):
+        across(k, z).wait_recv()
+        both_ways(k, other)
+
+    def forward(k, apart, side):
         @pl.when(z >= apart)
         def _():
-            source = z - apart
-            rightward(k, source).wait_recv()
-            pl.when(z < outer - 1)(lambda: rightward(k, source).start())
-            across(k, source).start()
+            chunk = (z - apart) * 2 + side
+            rightward(k, chunk).wait_recv()
+            pl.when(z < outer - 1)(lambda: rightward(k, chunk).start())
+            if k >= x_first:
+                across(k, z - apart).start()
 
         @pl.when(z + apart < outer)
         def _():
-            source = z + apart
-            leftward(k, source).wait_recv()
-            pl.when(z > 0)(lambda: leftward(k, source).start())
-            across(k, source).start()
-
-    for tick in range(pieces + outer):
+            chunk = (z + apart) * 2 + side
+            leftward(k, chunk).wait_recv()
+            pl.when(z > 0)(lambda: leftward(k, chunk).start())
+            if k >= x_first:
+                across(k, z + apart).start()
+
+    for k in range(min(2, pieces)):
+        send_pairs(k)
+    for tick in range(pieces + outer + 2):
         if tick < pieces:
             pair_sums(tick)
         if 0 <= tick - 1 < pieces:
             update(tick - 1)
+        if tick + 2 < pieces:
+            send_pairs(tick + 2)
+        if tick < pieces:
+            merges(tick)
+        if 0 <= tick - 3 < x_first:
+            from_partner(tick - 3)
         for apart in range(1, outer):
             if 0 <= tick - 1 - apart < pieces:
-                forward(tick - 1 - apart, apart)
-
-    for group in (xs, zs):
-        for copy in group.values():
-            copy.wait_send()
+                forward(tick - 1 - apart, apart, x)
+            if 0 <= tick - 3 - apart < x_first:
+                forward(tick - 3 - apart, apart, 1 - x)
+
+    for copy in xs.values():
+        copy.wait_send()
     for k in range(pieces):
+        for step in range(outer):
+            pl.when(step != given)(lambda: to_pair(k, step).wait_send())
         for source in range(outer):
+            for side in (x, 1 - x) if k < x_first else (x,):
+                chunk = source * 2 + side
+                pl.when((source <= z) & (z < outer - 1))(lambda: rightward(k, chunk).wait_send())
+                pl.when((source >= z) & (z > 0))(lambda: leftward(k, chunk).wait_send())
+        for source in (z,) if k < x_first else range(outer):
             across(k, source).wait_send()
-            pl.when((source <= z) & (z < outer - 1))(lambda: rightward(k, source).wait_send())
-            pl.when((source >= z) & (z > 0))(lambda: leftward(k, source).wait_send())
-    for k in range(pieces):
+    for k in range(x_first, pieces):
         for source in range(outer):
             across(k, source).wait_recv()
 
@@ -229,15 +291,16 @@
         scratch_shapes=[
             pltpu.VMEM((pieces, outer, ROWS, width), bf16),
             pltpu.VMEM((pieces, outer, ROWS, width), bf16),
-            pltpu.VMEM((pieces, outer - 1, ROWS, width), bf16),
+            pltpu.VMEM((pieces, outer, ROWS, width), bf16),
             pltpu.VMEM((pieces, ROWS, width), f32),
-            pltpu.VMEM((pieces, outer - 1, ROWS, width), bf16),
+            pltpu.VMEM((pieces, outer, ROWS, width), bf16),
+            pltpu.VMEM((pieces, outer // 2, ROWS, width), bf16),
             pltpu.VMEM(state, f32), pltpu.VMEM(state, bf16), pltpu.VMEM(state, bf16),
             pltpu.VMEM((1, owned), f32), pltpu.VMEM((1, owned), f32),
             dma((pieces, outer)), dma((5,)),
             dma((pieces, outer)), dma((pieces, outer)),
-            dma((pieces, outer - 1)), dma((pieces, outer - 1)),
-            dma((pieces, outer)), dma((pieces, outer)), dma((pieces, outer)),
+            dma((pieces, outer)), dma((pieces, outer)), dma((pieces, outer // 2)),
+            dma((pieces, 2 * outer)), dma((pieces, 2 * outer)), dma((pieces, 2 * outer)),
             dma((pieces, outer)), dma((pieces, outer)),
         ],
         compiler_params=pltpu.CompilerParams(

time: 56.1 us -> 60.8 us (1.084)
  Pallas kernels: 55.3 us -> 60 us
    pallas_call x1, Pallas kernels: 53.6 us -> 58.2 us  [per_device(): pl.pallas_call(functools.partial(kernel, outer), out_shape=tuple((pltpu.V...]
where the time goes in v3:
time: 60.8 us; the launch traced here: 60.6 us
  Pallas kernels  60 us (99%)
  between operations  0.64 us (1%)
    pallas_call x1, Pallas kernels, per_device(): pl.pallas_call(functools.partial(kernel, outer), out_shape=tuple((pltpu.V...  58.2 us
    pallas_call x1, Pallas kernels, per_device(): pl.pallas_call(write_out, out_shape=tuple((shape(*each) for each in out_s...  1.73 us

profile of v3, /device:TPU:0, one launch (start us, length us, event | category | flops | bytes accessed | tf_op | source)
XLA Modules:
  0.0 60.6 jit_solution(935276048727258182)
XLA Ops:
  0.6 58.2 %shard_map.109 = (f32[1,512,256]{2,1,0:T(8,128)S(1)}, bf16[1,512,256]{2,1,0:T(8,128)(2,1)S(1)}, f32[1,512]{1,0:T(1,128)S(1)}, bf16[1,512,256]{2,1,0:T(8,128)(2,1...) custom-call(bf16[1,1,4096,256]{3,2,1,0:T(8,128)(2,1)} %grads.1, f32[1,512,256]{2,1,0:T(8,128)} %master.1, ...), custom_call_target="tpu_custom_call" | custom-call | tf_op jit(solution)/shard_map/pallas_call | solution.py:286
  58.9 1.7 %shard_map.110 = (f32[1,512,256]{2,1,0:T(8,128)}, bf16[1,512,256]{2,1,0:T(8,128)(2,1)}, f32[1,512]{1,0:T(1,128)}, bf16[1,512,256]{2,1,0:T(8,128)(2,1)}, f32[1,512]{1,0:T(1,128)}, /*index=5*/bf16[1,4096,256]{2,1,0:T(8,128)(2,1)}) custom-call(f32[1,512,256]{2,1,0:T(8,128)S(1)} %get-tuple-element.12.refs_0_, ...), custom_call_target="tpu_custom_call" | custom-call | tf_op jit(solution)/shard_map/pallas_call | solution.py:311
